TPU v7x, 32 devices: a whole 2x2x4 slice. The times are simulated.
32 devices in a mesh: state: 2 (over x), bond: 16 (over z, y, core).
Axes of the slice: x: 2, y: 2, z: 4, core: 2. Of those that a mesh axis runs over, the one named last changes fastest.
Arguments:
- intersect_left: bfloat16 [2, 2048, 2048], P('state', 'bond'), may hold values from -0.125 to 0.125
- stored_block: bfloat16 [2, 4, 2048, 2048], P('state', None, 'bond'), may hold values from -6 to 6
- stored_site: bfloat16 [2, 2, 2048, 2048], P('state', None, 'bond'), may hold values from -6 to 6
- current_site: bfloat16 [2048, 2, 2048], P('bond', None, 'state'), may hold values from -0.09375 to 0.09375
- current_block: bfloat16 [4, 2048, 2048], P(None, 'bond', 'state'), may hold values from -6 to 6
- penalty_weight: float32 [2], replicated, may hold values from 0.5 to 4
Outputs:
- penalized: float32 [4, 2048, 2048], P(None, 'bond', 'state')
- intersect_next: bfloat16 [2, 2048, 2048], P('state', 'bond')
All inputs are finite; a program needn't handle non-finite values.
Results may differ from a plain program's by a relative error of at most 0.0055.
Values may be sent and summed in bfloat16 or wider, within the bound.
A program may use at most 64 MiB of HBM per device.

v0:
```python
import jax
import jax.numpy as jnp
from jax import lax
from jax.sharding import PartitionSpec as P


def contract_last(left, right):
    return lax.dot_general(
        left, right, (((1,), (1,)), ((), ())), preferred_element_type=jnp.float32
    )


def shards(intersect_left, stored_block, stored_site, current_site, current_block, penalty_weight):
    bond_width = intersect_left.shape[2]
    column_count = stored_block.shape[2]
    pair_count = stored_block.shape[1]
    physical = stored_site.shape[1]
    operand = jnp.concatenate(
        [
            stored_block[0].reshape(pair_count * column_count, bond_width),
            stored_site[0].reshape(physical * column_count, bond_width),
        ],
        axis=0,
    )
    products = contract_last(operand, lax.all_gather(intersect_left, "bond", axis=1, tiled=True)[0])
    projected = products[: pair_count * column_count].reshape(pair_count, column_count, bond_width)
    moved = (
        products[pair_count * column_count :]
        .astype(jnp.bfloat16)
        .reshape(1, physical, column_count, bond_width)
    )
    scale_factor = 1.0 / (physical * bond_width)
    whole_block = lax.all_gather(current_block, "state", axis=2, tiled=True)
    intersect = (
        lax.psum(jnp.sum(projected * whole_block.astype(jnp.float32)), "bond") * scale_factor
    )
    weight = penalty_weight[lax.axis_index("state")]
    summed = lax.psum_scatter(
        weight * intersect * projected, "state", scatter_dimension=2, tiled=True
    )
    penalized = current_block.astype(jnp.float32) + summed
    moved_all = lax.all_gather(moved, "state", axis=0, tiled=True)
    grown = jnp.einsum(
        "asf,ksea->kfe",
        lax.all_gather(current_site, "bond", axis=0, tiled=True),
        moved_all,
        preferred_element_type=jnp.float32,
    )
    intersect_next = lax.all_to_all(
        lax.all_to_all(
            grown.astype(jnp.bfloat16), "state", split_axis=0, concat_axis=1, tiled=True
        ),
        "bond",
        split_axis=1,
        concat_axis=2,
        tiled=True,
    )
    return (penalized, intersect_next)


def solution(mesh):
    placed = (
        P("state", "bond", None),
        P("state", None, "bond", None),
        P("state", None, "bond", None),
        P("bond", None, "state"),
        P(None, "bond", "state"),
        P(),
    )
    return jax.shard_map(
        shards,
        mesh=mesh,
        in_specs=placed,
        out_specs=(P(None, "bond", "state"), P("state", "bond", None)),
        check_vma=False,
    )
```

profile of v0, /device:TPU:0, one launch (start us, length us, event | category | flops | bytes accessed | tf_op | source)
XLA Modules:
  0.0 307.0 jit_solution(15348684443080593336)
XLA Ops:
  7.2 0.0 all-gather.5.cloned.1.call-start
  7.2 0.7 all-gather.5.cloned.1.call-update
  7.9 0.0 all-gather.7.cloned.1.call-start
  7.9 0.7 all-gather.7.cloned.1.call-update
  8.6 0.0 all-gather.11.cloned.1.call-start
  8.7 2.0 copy.15
  10.6 0.0 all-gather.11.cloned.1.call-update
  10.7 0.0 all-gather.9.cloned.1.call-start
  10.7 76.5 %all-gather.5.cloned.1.call-done = bf16[1,2048,2048]{2,1,0:T(8,128)(2,1)} async-done(((bf16[1,128,2048]{2,1,0:T(8,128)(2,1)}), bf16[1,2048,2048]{2,1,0:T(8,128)(2,1)}) %all-gather.5.cloned.1.call-update) | async-done | bytes 8388624 | tf_op jit(solution)/shard_map/all_gather | solution.py:25
  87.2 10.1 %fusion.2 = f32[768,2048]{1,0:T(8,128)S(1)} fusion(bf16[1,2048,2048]{2,1,0:T(8,128)(2,1)} %all-gather.5.cloned.1.call-done, bf16[256,2048]{1,0:T(8,128)(2,1)} %bitcast.45, bf16[512,2048]{1,0:T(8,128)(2,1)} %bitcast.44), kind=kOutput, calls=%fused_computation.2 | convolution fusion | flops 6448742400 | bytes 17825792 | tf_op jit(solution)/shard_map/dot_general | solution.py:8
  97.3 0.0 copy-start
  97.3 2.7 copy-done
  100.0 1.1 slice.13
  101.1 0.0 all-gather.9.cloned.1.call-update
  101.1 0.0 reduce-scatter.2.cloned.1.call-start
  101.2 4.7 %slice.9 = f32[512,2048]{1,0:T(8,128)} slice(f32[768,2048]{1,0:T(8,128)} %copy-done), slice={[0:512], [0:2048]} | slice | bytes 8388608 | tf_op jit(solution)/shard_map/slice | solution.py:26
  105.9 0.0 copy-start.2
  105.9 14.6 %all-gather.7.cloned.1.call-done = bf16[4,128,2048]{2,1,0:T(8,128)(2,1)} async-done(((bf16[4,128,1024]{2,1,0:T(8,128)(2,1)}), bf16[4,128,2048]{2,1,0:T(8,128)(2,1)}) %all-gather.7.cloned.1.call-update) | async-done | bytes 2097168 | tf_op jit(solution)/shard_map/all_gather | solution.py:33
  120.4 4.6 %multiply_reduce_fusion = f32[]{:T(128)} fusion(f32[4,128,2048]{2,1,0:T(8,128)} %bitcast.37, bf16[4,128,2048]{2,1,0:T(8,128)(2,1)} %all-gather.7.cloned.1.call-done), kind=kLoop, calls=%fused_computation.4 | loop fusion | flops 3145727 | bytes 6291460 | tf_op jit(solution)/shard_map/reduce_sum | solution.py:35
  125.0 0.0 copy-done.2
  125.0 0.6 dynamic_slice.3
  125.7 34.8 %psum.7 = f32[]{:T(128)} all-reduce(f32[]{:T(128)} %multiply_reduce_fusion), channel_id=1, replica_groups=mesh['state'=2,'bond'=16] {'bond'}, use_global_device_ids=true, to_apply=%region_1.0 | all-reduce | flops 1 | bytes 8 | tf_op jit(solution)/shard_map/psum | solution.py:35
  161.7 4.8 %broadcast_multiply_fusion = f32[4,128,2048]{2,1,0:T(8,128)} fusion(f32[]{:T(128)S(6)} %mul.17, f32[768,2048]{1,0:T(8,128)} %copy-done), kind=kLoop, calls=%fused_computation.9 | loop fusion | flops 1048576 | bytes 8388612 | tf_op jit(solution)/shard_map/mul | solution.py:39
  166.5 0.0 reduce-scatter.2.cloned.1.call-update
  166.5 31.4 %all-gather.11.cloned.1.call-done = bf16[2048,2,1024]{2,0,1:T(8,128)(2,1)} async-done(((bf16[128,2,1024]{2,0,1:T(8,128)(2,1)}), bf16[2048,2,1024]{2,0,1:T(8,128)(2,1)}) %all-gather.11.cloned.1.call-update) | async-done | bytes 8388624 | tf_op jit(solution)/shard_map/all_gather | solution.py:45
  197.9 33.7 %all-gather.9.cloned.1.call-done = bf16[2,2,128,2048]{3,2,1,0:T(8,128)(2,1)} async-done(((bf16[1,2,128,2048]{3,2,1,0:T(8,128)(2,1)}), bf16[2,2,128,2048]{3,2,1,0:T(8,128)(2,1)}) %all-gather.9.cloned.1.call-update) | async-done | bytes 2097168 | tf_op jit(solution)/shard_map/all_gather | solution.py:42
  231.5 6.3 %fusion.13 = bf16[2,1024,128]{1,2,0:T(8,128)(2,1)S(1)} fusion(bf16[2,2,128,2048]{3,2,1,0:T(8,128)(2,1)} %all-gather.9.cloned.1.call-done, bf16[2048,2,1024]{2,0,1:T(8,128)(2,1)} %all-gather.11.cloned.1.call-done), kind=kOutput, calls=%fused_computation.13 | convolution fusion | flops 2147745792 | bytes 11010048 | tf_op jit(solution)/shard_map/asf,ksea->kfe/dot_general | solution.py:43
  237.9 17.0 %all_to_all.30 = bf16[2,1024,128]{1,2,0:T(8,128)(2,1)S(1)} all-to-all(bf16[2,1024,128]{1,2,0:T(8,128)(2,1)S(1)} %fusion.13), channel_id=1, replica_groups=mesh['state'=2,'bond'=16] {'state'}, dimensions={0} | all-to-all | bytes 1048576 | tf_op jit(solution)/shard_map/all_to_all | solution.py:50
  254.8 0.3 copy.16
  255.1 8.1 %copy.23 = bf16[1,2048,128]{2,0,1:T(2,128)(2,1)S(1)} copy(bf16[1,2048,128]{2,1,0:T(8,128)(2,1)S(1)} %bitcast.41) | data formatting | bytes 1048576 | tf_op jit(solution)/shard_map/all_to_all | solution.py:50
  263.3 0.5 broadcast
  263.8 0.0 copy-start.1
  263.8 11.6 %reduce = bf16[2048,128]{1,0:T(8,128)(2,1)S(1)} reduce(bf16[2048,1,128]{2,1,0:T(2,128)(2,1)S(1)} %bitcast.40, bf16[]{:T(256)} %broadcast), dimensions={1}, to_apply=%bitcast.36.reduce_sub_computation | reduce | bytes 1048578
  275.4 0.1 reshape.17
  275.5 19.7 %all_to_all.31 = bf16[16,2,8192]{2,1,0:T(2,128)(2,1)S(1)} all-to-all(bf16[16,2,8192]{2,1,0:T(2,128)(2,1)S(1)} %reshape.17), channel_id=1, replica_groups=mesh['state'=2,'bond'=16] {'bond'}, dimensions={0} | all-to-all | bytes 1048576 | tf_op jit(solution)/shard_map/all_to_all | solution.py:49
  295.2 0.5 reshape.18
  295.7 0.1 copy.21
  295.8 0.3 copy.18
  296.1 1.0 copy.19
  297.1 0.0 reduce-scatter.2.cloned.1.call-done
  297.1 0.0 copy-done.1
  297.1 3.4 %convert_add_fusion = f32[4,128,1024]{2,1,0:T(8,128)} fusion(f32[4,128,1024]{2,1,0:T(8,128)} %reduce-scatter.2.cloned.1.call-done, bf16[4,128,1024]{2,1,0:T(8,128)(2,1)S(1)} %copy-done.1), kind=kLoop, calls=%fused_computation.10 | loop fusion | flops 1048576 | bytes 5242880 | tf_op jit(solution)/shard_map/add | solution.py:41
Async XLA Ops:
  7.2 80.0 %all-gather.5.cloned.1.call-start = ((), (), s32[]{:S(2)}) async-start(), calls=%async_computation.3 | async-start | bytes 8912896 | tf_op jit(solution)/shard_map/all_gather | solution.py:25
  7.9 112.5 %all-gather.7.cloned.1.call-start = ((), (), s32[]{:S(2)}) async-start(), calls=%async_computation.4 | async-start | bytes 3145728 | tf_op jit(solution)/shard_map/all_gather | solution.py:33
  8.6 189.2 %all-gather.11.cloned.1.call-start = ((), (), s32[]{:S(2)}) async-start(), calls=%async_computation.7 | async-start | bytes 8912896 | tf_op jit(solution)/shard_map/all_gather | solution.py:45
  10.7 220.9 %all-gather.9.cloned.1.call-start = ((), (), s32[]{:S(2)}) async-start(), calls=%async_computation.6 | async-start | bytes 3145728 | tf_op jit(solution)/shard_map/all_gather | solution.py:42
  97.3 2.7 copy-start
  101.1 196.0 %reduce-scatter.2.cloned.1.call-start = ((), (), s32[]{:S(2)}) async-start(), calls=%async_computation.5 | async-start | bytes 6291456 | tf_op jit(solution)/shard_map/reduce_scatter | solution.py:38
  105.9 19.2 %copy-start.2 = (f32[2]{0:T(128)S(1)}, f32[2]{0:T(128)}, u32[]{:S(2)}) copy-start(f32[2]{0:T(128)} %param.11) | copy-start | bytes 28
  263.8 33.3 %copy-start.1 = (bf16[4,128,1024]{2,1,0:T(8,128)(2,1)S(1)}, bf16[4,128,1024]{2,1,0:T(8,128)(2,1)}, u32[]{:S(2)}) copy-start(bf16[4,128,1024]{2,1,0:T(8,128)(2,1)} %param.10) | copy-start | bytes 3145732
Sparse Core Ops, SparseCore 0:
  10.1 77.0 all-gather.4
  88.7 31.6 all-gather.6
  123.2 74.6 all-gather.10
  199.8 31.6 all-gather.8
  233.7 59.9 reduce-scatter.1
where the time goes:
time: 307 us
  waiting for transfers between devices  158 us (51%)
  blocking collectives  71.4 us (23%)
  other arithmetic  24.3 us (8%)
  local copies, waits for them, and re-layouts  22 us (7%)
  matrix products  16.5 us (5%)
  between operations  15.1 us (5%)
    all_gather x1, waiting for transfers between devices, shards(): lax.all_gather(intersect_left, 'bond', axis=1, tiled=True)[0]  76.5 us
    psum x1, blocking collectives, shards(): lax.psum(jnp.sum(projected * whole_block.astype(jnp.float32)), 'bond')  34.8 us
    all_gather x1, waiting for transfers between devices, shards(): moved_all = lax.all_gather(moved, 'state', axis=0, tiled=True)  33.7 us
    all_gather x1, waiting for transfers between devices, shards(): lax.all_gather(current_site, 'bond', axis=0, tiled=True)  31.4 us
    all_to_all x1, blocking collectives, shards(): lax.all_to_all(lax.all_to_all(grown.astype(jnp.bfloat16), 'state', split_...  19.7 us
    all_to_all x1, blocking collectives, shards(): lax.all_to_all(grown.astype(jnp.bfloat16), 'state', split_axis=0, concat_...  17 us
    all_gather x1, waiting for transfers between devices, shards(): whole_block = lax.all_gather(current_block, 'state', axis=2, tiled=True)  14.6 us
    unnamed x1, other arithmetic  11.6 us
  transfers between devices with their start and end apart: 5, of which 4 were waited for; matrix products, arithmetic and copies ran while one was open for 18% of the time, Pallas kernels for 0%

commit v1 on v0

--- a/solution.py
+++ b/solution.py
@@ -40,12 +40,39 @@
     )
     penalized = current_block.astype(jnp.float32) + summed
     moved_all = lax.all_gather(moved, "state", axis=0, tiled=True)
+    z, mid_arr, e_now = (lax.axis_size("bond"), lax.axis_index("bond"), current_site.shape[0])
+    queue = [(j0, (j0 + 1) % z) for j0 in range(z)]
+    so_far_all = [(j0, (j0 - 1) % z) for j0 in range(z)]
+    kept_arr = z // 2
+    local_next = w_next = current_site
     grown = jnp.einsum(
         "asf,ksea->kfe",
-        lax.all_gather(current_site, "bond", axis=0, tiled=True),
-        moved_all,
+        current_site,
+        lax.dynamic_slice_in_dim(moved_all, mid_arr * e_now, current_site.shape[0], axis=3),
         preferred_element_type=jnp.float32,
     )
+    nth = 1
+    while nth < kept_arr + 1:
+        local_next = lax.ppermute(local_next, axis_name="bond", perm=queue)
+        if nth < z - kept_arr:
+            w_next = lax.ppermute(w_next, axis_name="bond", perm=so_far_all)
+            grown = grown + jnp.einsum(
+                "asf,ksea->kfe",
+                w_next,
+                lax.dynamic_slice_in_dim(
+                    moved_all, (mid_arr + nth) % z * e_now, w_next.shape[0], axis=3
+                ),
+                preferred_element_type=jnp.float32,
+            )
+        grown = grown + jnp.einsum(
+            "asf,ksea->kfe",
+            local_next,
+            lax.dynamic_slice_in_dim(
+                moved_all, (mid_arr - nth) % z * e_now, local_next.shape[0], axis=3
+            ),
+            preferred_element_type=jnp.float32,
+        )
+        nth += 1
     intersect_next = lax.all_to_all(
         lax.all_to_all(
             grown.astype(jnp.bfloat16), "state", split_axis=0, concat_axis=1, tiled=True

time: 307 us -> 326 us (1.062)
  starting transfers between devices: 0.2 us -> 54.3 us
  waiting for transfers between devices: 158 us -> 123 us
  blocking collectives: 71.4 us -> 65.4 us
  matrix products: 16.5 us -> 20.6 us
    ppermute x0 -> x15, starting transfers between devices: none -> 54.1 us  [the longest x8 41.6 us: shards(): local_next = lax.ppermute(local_next, axis_name='bond', perm=queue)]
    all_gather x1, waiting for transfers between devices: 33.7 us -> 0.01 us  [shards(): moved_all = lax.all_gather(moved, 'state', axis=0, tiled=True)]
    all_gather x1 -> x0, waiting for transfers between devices: 31.4 us -> none  [shards(): lax.all_gather(current_site, 'bond', axis=0, tiled=True)]
    ppermute x0 -> x15, waiting for transfers between devices: none -> 28.6 us  [the longest x8 16.6 us: shards(): local_next = lax.ppermute(local_next, axis_name='bond', perm=queue)]
    all_to_all x1, blocking collectives: 17 us -> 10.3 us  [shards(): lax.all_to_all(grown.astype(jnp.bfloat16), 'state', split_axis=0, concat_...]
    dot_general x1 -> x16, matrix products: 6.34 us -> 10.5 us  [the longest x7 5.36 us: shards(): jnp.einsum('asf,ksea->kfe', w_next, lax.dynamic_slice_in_dim(moved_all, (...]
    unnamed x12 -> x40, local copies, waits for them, and re-layouts: 6.89 us -> 7.58 us
  transfers between devices with their start and end apart: 5 -> 19, of which waited for: 4 -> 10; matrix products, arithmetic and copies ran while one was open for 18% -> 18% of each run, Pallas kernels for 0% -> 0%
where the time goes in v1:
time: 326 us; the launch traced here: 325 us
  waiting for transfers between devices  123 us (38%)
  blocking collectives  65.4 us (20%)
  starting transfers between devices  54.3 us (17%)
  other arithmetic  24.3 us (7%)
  local copies, waits for them, and re-layouts  22.7 us (7%)
  matrix products  20.6 us (6%)
  between operations  15.4 us (5%)
    all_gather x1, waiting for transfers between devices, shards(): lax.all_gather(intersect_left, 'bond', axis=1, tiled=True)[0]  78.5 us
    ppermute x8, starting transfers between devices, shards(): local_next = lax.ppermute(local_next, axis_name='bond', perm=queue)  41.6 us
    psum x1, blocking collectives, shards(): lax.psum(jnp.sum(projected * whole_block.astype(jnp.float32)), 'bond')  33.7 us
    all_to_all x1, blocking collectives, shards(): lax.all_to_all(lax.all_to_all(grown.astype(jnp.bfloat16), 'state', split_...  21.4 us
    ppermute x8, waiting for transfers between devices, shards(): local_next = lax.ppermute(local_next, axis_name='bond', perm=queue)  16.6 us
    all_gather x1, waiting for transfers between devices, shards(): whole_block = lax.all_gather(current_block, 'state', axis=2, tiled=True)  14.1 us
    ppermute x7, starting transfers between devices, shards(): w_next = lax.ppermute(w_next, axis_name='bond', perm=so_far_all)  12.5 us
    ppermute x7, waiting for transfers between devices, shards(): w_next = lax.ppermute(w_next, axis_name='bond', perm=so_far_all)  12 us
  transfers between devices with their start and end apart: 19, of which 10 were waited for; matrix products, arithmetic and copies ran while one was open for 18% of the time, Pallas kernels for 0%

profile of v1, /device:TPU:0, one launch (start us, length us, event | category | flops | bytes accessed | tf_op | source)
XLA Modules:
  0.0 325.3 jit_solution(3569771426711832778)
XLA Ops:
  7.2 0.7 all-gather.4.cloned.1.call-update
  7.9 0.7 all-gather.6.cloned.1.call-update
  8.7 78.5 %all-gather.4.cloned.1.call-done = bf16[1,2048,2048]{2,1,0:T(8,128)(2,1)} async-done(((bf16[1,128,2048]{2,1,0:T(8,128)(2,1)}), bf16[1,2048,2048]{2,1,0:T(8,128)(2,1)}) %all-gather.4.cloned.1.call-update) | async-done | bytes 8388624 | tf_op jit(solution)/shard_map/all_gather | solution.py:25
  87.2 10.1 %fusion = f32[768,2048]{1,0:T(8,128)S(1)} fusion(bf16[1,2048,2048]{2,1,0:T(8,128)(2,1)} %all-gather.4.cloned.1.call-done, bf16[256,2048]{1,0:T(8,128)(2,1)} %bitcast.158, bf16[512,2048]{1,0:T(8,128)(2,1)} %bitcast.157), kind=kOutput, calls=%fused_computation | convolution fusion | flops 6448742400 | bytes 17825792 | tf_op jit(solution)/shard_map/dot_general | solution.py:8
  97.3 2.6 copy-done
  99.9 1.1 slice.13
  101.1 0.1 copy.21
  101.2 0.3 collective-permute-start.1
  101.6 4.7 %slice.9 = f32[512,2048]{1,0:T(8,128)} slice(f32[768,2048]{1,0:T(8,128)} %copy-done), slice={[0:512], [0:2048]} | slice | bytes 8388608 | tf_op jit(solution)/shard_map/slice | solution.py:26
  106.3 14.1 %all-gather.6.cloned.1.call-done = bf16[4,128,2048]{2,1,0:T(8,128)(2,1)} async-done(((bf16[4,128,1024]{2,1,0:T(8,128)(2,1)}), bf16[4,128,2048]{2,1,0:T(8,128)(2,1)}) %all-gather.6.cloned.1.call-update) | async-done | bytes 2097168 | tf_op jit(solution)/shard_map/all_gather | solution.py:33
  120.4 4.6 %multiply_reduce_fusion = f32[]{:T(128)} fusion(f32[4,128,2048]{2,1,0:T(8,128)} %bitcast.150, bf16[4,128,2048]{2,1,0:T(8,128)(2,1)} %all-gather.6.cloned.1.call-done), kind=kLoop, calls=%fused_computation.2 | loop fusion | flops 3145727 | bytes 6291460 | tf_op jit(solution)/shard_map/reduce_sum | solution.py:35
  125.1 0.6 dynamic_slice.51
  125.7 33.7 %psum.7 = f32[]{:T(128)} all-reduce(f32[]{:T(128)} %multiply_reduce_fusion), channel_id=1, replica_groups=mesh['state'=2,'bond'=16] {'bond'}, use_global_device_ids=true, to_apply=%region_1.0 | all-reduce | flops 1 | bytes 8 | tf_op jit(solution)/shard_map/psum | solution.py:35
  160.7 4.8 %broadcast_multiply_fusion = f32[4,128,2048]{2,1,0:T(8,128)} fusion(f32[]{:T(128)S(6)} %mul.65, f32[768,2048]{1,0:T(8,128)} %copy-done), kind=kLoop, calls=%fused_computation.7 | loop fusion | flops 1048576 | bytes 8388612 | tf_op jit(solution)/shard_map/mul | solution.py:39
  165.6 0.5 collective-permute-start.3
  166.0 6.2 %collective-permute-done = bf16[128,2,1024]{2,0,1:T(8,128)(2,1)S(1)} collective-permute-done((bf16[128,2,1024]{2,0,1:T(8,128)(2,1)S(1)}, bf16[128,2,1024]{2,0,1:T(8,128)(2,1)S(1)}, u32[]{:S(2)}, u32[]{:S(2)}) %collective-permute-start) | collective-permute-done | bytes 524320 | tf_op jit(solution)/shard_map/ppermute | solution.py:58
  172.2 4.6 %collective-permute-start.2 = (bf16[128,2,1024]{2,0,1:T(8,128)(2,1)S(1)}, bf16[128,2,1024]{2,0,1:T(8,128)(2,1)S(1)}, u32[]{:S(2)}, u32[]{:S(2)}) collective-permute-start(bf16[128,2,1024]{2,0,1:T(8,128)(2,1)S(1)} %collective-permute-done), channel_id=1, source_target_pairs={{0,15},{1,0},{2,1},{3,2},{4,3},{5,4},{6,5},{7,6},{8,7},{9,8},{10,9... | collective-permute-start | bytes 1572872 | tf_op jit(solution)/shard_map/ppermute | solution.py:58
  176.8 0.2 collective-permute-done.3
  177.0 0.8 collective-permute-start.5
  177.8 5.8 %collective-permute-done.2 = bf16[128,2,1024]{2,0,1:T(8,128)(2,1)S(1)} collective-permute-done((bf16[128,2,1024]{2,0,1:T(8,128)(2,1)S(1)}, bf16[128,2,1024]{2,0,1:T(8,128)(2,1)S(1)}, u32[]{:S(2)}, u32[]{:S(2)}) %collective-permute-start.2) | collective-permute-done | bytes 524320 | tf_op jit(solution)/shard_map/ppermute | solution.py:58
  183.5 4.7 %collective-permute-start.4 = (bf16[128,2,1024]{2,0,1:T(8,128)(2,1)S(1)}, bf16[128,2,1024]{2,0,1:T(8,128)(2,1)S(1)}, u32[]{:S(2)}, u32[]{:S(2)}) collective-permute-start(bf16[128,2,1024]{2,0,1:T(8,128)(2,1)S(1)} %collective-permute-done.2), channel_id=1, source_target_pairs={{0,15},{1,0},{2,1},{3,2},{4,3},{5,4},{6,5},{7,6},{8,7},{9,8},{10,9... | collective-permute-start | bytes 1572872 | tf_op jit(solution)/shard_map/ppermute | solution.py:58
  188.3 0.2 collective-permute-done.5
  188.4 8.2 %collective-permute-start.7 = (bf16[128,2,1024]{2,0,1:T(8,128)(2,1)S(1)}, bf16[128,2,1024]{2,0,1:T(8,128)(2,1)S(1)}, u32[]{:S(2)}, u32[]{:S(2)}) collective-permute-start(bf16[128,2,1024]{2,0,1:T(8,128)(2,1)S(1)} %collective-permute-done.5), channel_id=1, source_target_pairs={{0,1},{1,2},{2,3},{3,4},{4,5},{5,6},{6,7},{7,8},{8,9},{9,10},{10,1... | collective-permute-start | bytes 1572872 | tf_op jit(solution)/shard_map/ppermute | solution.py:56
  196.6 3.0 collective-permute-start.6
  199.6 1.3 collective-permute-done.7
  201.0 9.9 %collective-permute-start.9 = (bf16[128,2,1024]{2,0,1:T(8,128)(2,1)S(1)}, bf16[128,2,1024]{2,0,1:T(8,128)(2,1)S(1)}, u32[]{:S(2)}, u32[]{:S(2)}) collective-permute-start(bf16[128,2,1024]{2,0,1:T(8,128)(2,1)S(1)} %collective-permute-done.7), channel_id=1, source_target_pairs={{0,1},{1,2},{2,3},{3,4},{4,5},{5,6},{6,7},{7,8},{8,9},{9,10},{10,1... | collective-permute-start | bytes 1572872 | tf_op jit(solution)/shard_map/ppermute | solution.py:56
  210.9 0.1 collective-permute-start.8
  211.0 4.7 %collective-permute-done.9 = bf16[128,2,1024]{2,0,1:T(8,128)(2,1)S(1)} collective-permute-done((bf16[128,2,1024]{2,0,1:T(8,128)(2,1)S(1)}, bf16[128,2,1024]{2,0,1:T(8,128)(2,1)S(1)}, u32[]{:S(2)}, u32[]{:S(2)}) %collective-permute-start.9) | collective-permute-done | bytes 524320 | tf_op jit(solution)/shard_map/ppermute | solution.py:56
  215.7 9.4 %collective-permute-start.11 = (bf16[128,2,1024]{2,0,1:T(8,128)(2,1)S(1)}, bf16[128,2,1024]{2,0,1:T(8,128)(2,1)S(1)}, u32[]{:S(2)}, u32[]{:S(2)}) collective-permute-start(bf16[128,2,1024]{2,0,1:T(8,128)(2,1)S(1)} %collective-permute-done.9), channel_id=1, source_target_pairs={{0,1},{1,2},{2,3},{3,4},{4,5},{5,6},{6,7},{7,8},{8,9},{9,10},{10,1... | collective-permute-start | bytes 1572872 | tf_op jit(solution)/shard_map/ppermute | solution.py:56
  225.1 5.2 %collective-permute-done.11 = bf16[128,2,1024]{2,0,1:T(8,128)(2,1)S(1)} collective-permute-done((bf16[128,2,1024]{2,0,1:T(8,128)(2,1)S(1)}, bf16[128,2,1024]{2,0,1:T(8,128)(2,1)S(1)}, u32[]{:S(2)}, u32[]{:S(2)}) %collective-permute-start.11) | collective-permute-done | bytes 524320 | tf_op jit(solution)/shard_map/ppermute | solution.py:56
  230.3 9.1 %collective-permute-start.13 = (bf16[128,2,1024]{2,0,1:T(8,128)(2,1)S(1)}, bf16[128,2,1024]{2,0,1:T(8,128)(2,1)S(1)}, u32[]{:S(2)}, u32[]{:S(2)}) collective-permute-start(bf16[128,2,1024]{2,0,1:T(8,128)(2,1)S(1)} %collective-permute-done.11), channel_id=1, source_target_pairs={{0,1},{1,2},{2,3},{3,4},{4,5},{5,6},{6,7},{7,8},{8,9},{9,10},{10,1... | collective-permute-start | bytes 1572872 | tf_op jit(solution)/shard_map/ppermute | solution.py:56
  239.5 5.1 %collective-permute-done.13 = bf16[128,2,1024]{2,0,1:T(8,128)(2,1)S(1)} collective-permute-done((bf16[128,2,1024]{2,0,1:T(8,128)(2,1)S(1)}, bf16[128,2,1024]{2,0,1:T(8,128)(2,1)S(1)}, u32[]{:S(2)}, u32[]{:S(2)}) %collective-permute-start.13) | collective-permute-done | bytes 524320 | tf_op jit(solution)/shard_map/ppermute | solution.py:56
  244.6 3.4 %collective-permute-start.14 = (bf16[128,2,1024]{2,0,1:T(8,128)(2,1)S(1)}, bf16[128,2,1024]{2,0,1:T(8,128)(2,1)S(1)}, u32[]{:S(2)}, u32[]{:S(2)}) collective-permute-start(bf16[128,2,1024]{2,0,1:T(8,128)(2,1)S(1)} %collective-permute-done.13), channel_id=1, source_target_pairs={{0,1},{1,2},{2,3},{3,4},{4,5},{5,6},{6,7},{7,8},{8,9},{9,10},{10,1... | collective-permute-start | bytes 1572872 | tf_op jit(solution)/shard_map/ppermute | solution.py:56
  248.0 1.6 convolution_bitcast_fusion.5
  249.6 1.4 convolution_bitcast_fusion.7
  251.0 0.3 convolution_bitcast_fusion.9
  251.3 0.3 convolution_bitcast_fusion.11
  251.6 0.3 convolution_bitcast_fusion.13
  252.0 0.3 convolution_bitcast_fusion.15
  252.3 0.4 copy-done.9
  252.7 0.3 fusion.6
  253.0 0.7 copy-done.11
  253.7 0.3 fusion.8
  254.0 0.7 copy-done.13
  254.8 0.3 fusion.10
  255.1 0.7 copy-done.15
  255.8 0.3 fusion.12
  256.1 1.4 fusion.14
  257.6 0.3 convolution_bitcast_fusion.3
  257.9 1.4 fusion.16
  259.2 0.3 convolution_bitcast_fusion.1
  259.6 1.4 fusion.18
  260.9 0.3 fusion.21
  261.2 10.3 %all_to_all.30 = bf16[2,1024,128]{1,2,0:T(8,128)(2,1)S(1)} all-to-all(bf16[2,1024,128]{1,2,0:T(8,128)(2,1)S(1)} %fusion.21), channel_id=1, replica_groups=mesh['state'=2,'bond'=16] {'state'}, dimensions={0} | all-to-all | bytes 1048576 | tf_op jit(solution)/shard_map/all_to_all | solution.py:77
  271.5 0.3 copy.24
  271.8 8.1 %copy.50 = bf16[1,2048,128]{2,0,1:T(2,128)(2,1)S(1)} copy(bf16[1,2048,128]{2,1,0:T(8,128)(2,1)S(1)} %bitcast.154) | data formatting | bytes 1048576 | tf_op jit(solution)/shard_map/all_to_all | solution.py:77
  279.9 0.5 broadcast.15
  280.5 11.5 %reduce = bf16[2048,128]{1,0:T(8,128)(2,1)S(1)} reduce(bf16[2048,1,128]{2,1,0:T(2,128)(2,1)S(1)} %bitcast.153, bf16[]{:T(256)} %broadcast.15), dimensions={1}, to_apply=%bitcast.149.reduce_sub_computation | reduce | bytes 1048578
  292.0 0.1 reshape.47
  292.1 21.4 %all_to_all.31 = bf16[16,2,8192]{2,1,0:T(2,128)(2,1)S(1)} all-to-all(bf16[16,2,8192]{2,1,0:T(2,128)(2,1)S(1)} %reshape.47), channel_id=1, replica_groups=mesh['state'=2,'bond'=16] {'bond'}, dimensions={0} | all-to-all | bytes 1048576 | tf_op jit(solution)/shard_map/all_to_all | solution.py:76
  313.5 0.5 reshape.48
  314.2 0.3 copy.26
  314.4 1.0 copy.27
  315.5 3.4 %convert_add_fusion = f32[4,128,1024]{2,1,0:T(8,128)} fusion(f32[4,128,1024]{2,1,0:T(8,128)} %reduce-scatter.2.cloned.1.call-done, bf16[4,128,1024]{2,1,0:T(8,128)(2,1)S(1)} %copy-done.1), kind=kLoop, calls=%fused_computation.8 | loop fusion | flops 1048576 | bytes 5242880 | tf_op jit(solution)/shard_map/add | solution.py:41
  (48 shorter events, 0.5 us)
Async XLA Ops:
  7.2 80.0 %all-gather.4.cloned.1.call-start = ((), (), s32[]{:S(2)}) async-start(), calls=%async_computation.3 | async-start | bytes 8912896 | tf_op jit(solution)/shard_map/all_gather | solution.py:25
  7.9 112.5 %all-gather.6.cloned.1.call-start = ((), (), s32[]{:S(2)}) async-start(), calls=%async_computation.4 | async-start | bytes 3145728 | tf_op jit(solution)/shard_map/all_gather | solution.py:33
  8.6 239.4 %all-gather.8.cloned.1.call-start = ((), (), s32[]{:S(2)}) async-start(), calls=%async_computation.6 | async-start | bytes 3145728 | tf_op jit(solution)/shard_map/all_gather | solution.py:42
  97.3 2.6 copy-start
  99.9 1.2 copy-start.3
  101.1 214.4 %reduce-scatter.2.cloned.1.call-start = ((), (), s32[]{:S(2)}) async-start(), calls=%async_computation.5 | async-start | bytes 6291456 | tf_op jit(solution)/shard_map/reduce_scatter | solution.py:38
  101.2 64.3 %collective-permute-start.1 = (bf16[128,2,1024]{2,0,1:T(8,128)(2,1)S(1)}, bf16[128,2,1024]{2,0,1:T(8,128)(2,1)S(1)}, u32[]{:S(2)}, u32[]{:S(2)}) collective-permute-start(bf16[128,2,1024]{2,0,1:T(8,128)(2,1)S(1)} %copy.21), channel_id=1, source_target_pairs={{0,1},{1,2},{2,3},{3,4},{4,5},{5,6},{6,7},{7,8},{8,9},{9,10},{10,1... | collective-permute-start | bytes 1572872 | tf_op jit(solution)/shard_map/ppermute | solution.py:56
  120.4 4.6 %copy-start.16 = (f32[2]{0:T(128)S(1)}, f32[2]{0:T(128)}, u32[]{:S(2)}) copy-start(f32[2]{0:T(128)} %param.11) | copy-start | bytes 28
  165.5 6.8 %collective-permute-start = (bf16[128,2,1024]{2,0,1:T(8,128)(2,1)S(1)}, bf16[128,2,1024]{2,0,1:T(8,128)(2,1)S(1)}, u32[]{:S(2)}, u32[]{:S(2)}) collective-permute-start(bf16[128,2,1024]{2,0,1:T(8,128)(2,1)S(1)} %copy.21), channel_id=1, source_target_pairs={{0,15},{1,0},{2,1},{3,2},{4,3},{5,4},{6,5},{7,6},{8,7},{9,8},{10,9... | collective-permute-start | bytes 1572872 | tf_op jit(solution)/shard_map/ppermute | solution.py:58
  165.6 11.5 %collective-permute-start.3 = (bf16[128,2,1024]{2,0,1:T(8,128)(2,1)S(1)}, bf16[128,2,1024]{2,0,1:T(8,128)(2,1)S(1)}, u32[]{:S(2)}, u32[]{:S(2)}) collective-permute-start(bf16[128,2,1024]{2,0,1:T(8,128)(2,1)S(1)} %collective-permute-done.1), channel_id=1, source_target_pairs={{0,1},{1,2},{2,3},{3,4},{4,5},{5,6},{6,7},{7,8},{8,9},{9,10},{10,1... | collective-permute-start | bytes 1572872 | tf_op jit(solution)/shard_map/ppermute | solution.py:56
  172.2 27.4 %copy-start.8 = (bf16[128,2,1024]{2,0,1:T(8,128)(2,1)}, bf16[128,2,1024]{2,0,1:T(8,128)(2,1)S(1)}, u32[]{:S(2)}) copy-start(bf16[128,2,1024]{2,0,1:T(8,128)(2,1)S(1)} %collective-permute-done) | copy-start | bytes 1572868
  172.2 11.3 %collective-permute-start.2 = (bf16[128,2,1024]{2,0,1:T(8,128)(2,1)S(1)}, bf16[128,2,1024]{2,0,1:T(8,128)(2,1)S(1)}, u32[]{:S(2)}, u32[]{:S(2)}) collective-permute-start(bf16[128,2,1024]{2,0,1:T(8,128)(2,1)S(1)} %collective-permute-done), channel_id=1, source_target_pairs={{0,15},{1,0},{2,1},{3,2},{4,3},{5,4},{6,5},{7,6},{8,7},{9,8},{10,9... | collective-permute-start | bytes 1572872 | tf_op jit(solution)/shard_map/ppermute | solution.py:58
  177.0 11.4 %collective-permute-start.5 = (bf16[128,2,1024]{2,0,1:T(8,128)(2,1)S(1)}, bf16[128,2,1024]{2,0,1:T(8,128)(2,1)S(1)}, u32[]{:S(2)}, u32[]{:S(2)}) collective-permute-start(bf16[128,2,1024]{2,0,1:T(8,128)(2,1)S(1)} %collective-permute-done.3), channel_id=1, source_target_pairs={{0,1},{1,2},{2,3},{3,4},{4,5},{5,6},{6,7},{7,8},{8,9},{9,10},{10,1... | collective-permute-start | bytes 1572872 | tf_op jit(solution)/shard_map/ppermute | solution.py:56
  183.5 46.7 %copy-start.10 = (bf16[128,2,1024]{2,0,1:T(8,128)(2,1)}, bf16[128,2,1024]{2,0,1:T(8,128)(2,1)S(1)}, u32[]{:S(2)}) copy-start(bf16[128,2,1024]{2,0,1:T(8,128)(2,1)S(1)} %collective-permute-done.2) | copy-start | bytes 1572868
  183.5 13.1 %collective-permute-start.4 = (bf16[128,2,1024]{2,0,1:T(8,128)(2,1)S(1)}, bf16[128,2,1024]{2,0,1:T(8,128)(2,1)S(1)}, u32[]{:S(2)}, u32[]{:S(2)}) collective-permute-start(bf16[128,2,1024]{2,0,1:T(8,128)(2,1)S(1)} %collective-permute-done.2), channel_id=1, source_target_pairs={{0,15},{1,0},{2,1},{3,2},{4,3},{5,4},{6,5},{7,6},{8,7},{9,8},{10,9... | collective-permute-start | bytes 1572872 | tf_op jit(solution)/shard_map/ppermute | solution.py:58
  188.4 12.6 %collective-permute-start.7 = (bf16[128,2,1024]{2,0,1:T(8,128)(2,1)S(1)}, bf16[128,2,1024]{2,0,1:T(8,128)(2,1)S(1)}, u32[]{:S(2)}, u32[]{:S(2)}) collective-permute-start(bf16[128,2,1024]{2,0,1:T(8,128)(2,1)S(1)} %collective-permute-done.5), channel_id=1, source_target_pairs={{0,1},{1,2},{2,3},{3,4},{4,5},{5,6},{6,7},{7,8},{8,9},{9,10},{10,1... | collective-permute-start | bytes 1572872 | tf_op jit(solution)/shard_map/ppermute | solution.py:56
  196.6 33.7 %copy-start.12 = (bf16[128,2,1024]{2,0,1:T(8,128)(2,1)}, bf16[128,2,1024]{2,0,1:T(8,128)(2,1)S(1)}, u32[]{:S(2)}) copy-start(bf16[128,2,1024]{2,0,1:T(8,128)(2,1)S(1)} %collective-permute-done.4) | copy-start | bytes 1572868
  196.6 14.2 %collective-permute-start.6 = (bf16[128,2,1024]{2,0,1:T(8,128)(2,1)S(1)}, bf16[128,2,1024]{2,0,1:T(8,128)(2,1)S(1)}, u32[]{:S(2)}, u32[]{:S(2)}) collective-permute-start(bf16[128,2,1024]{2,0,1:T(8,128)(2,1)S(1)} %collective-permute-done.4), channel_id=1, source_target_pairs={{0,15},{1,0},{2,1},{3,2},{4,3},{5,4},{6,5},{7,6},{8,7},{9,8},{10,9... | collective-permute-start | bytes 1572872 | tf_op jit(solution)/shard_map/ppermute | solution.py:58
  201.0 10.0 %copy-start.6 = (bf16[128,2,1024]{2,0,1:T(8,128)(2,1)}, bf16[128,2,1024]{2,0,1:T(8,128)(2,1)S(1)}, u32[]{:S(2)}) copy-start(bf16[128,2,1024]{2,0,1:T(8,128)(2,1)S(1)} %collective-permute-done.7) | copy-start | bytes 1572868
  201.0 14.7 %collective-permute-start.9 = (bf16[128,2,1024]{2,0,1:T(8,128)(2,1)S(1)}, bf16[128,2,1024]{2,0,1:T(8,128)(2,1)S(1)}, u32[]{:S(2)}, u32[]{:S(2)}) collective-permute-start(bf16[128,2,1024]{2,0,1:T(8,128)(2,1)S(1)} %collective-permute-done.7), channel_id=1, source_target_pairs={{0,1},{1,2},{2,3},{3,4},{4,5},{5,6},{6,7},{7,8},{8,9},{9,10},{10,1... | collective-permute-start | bytes 1572872 | tf_op jit(solution)/shard_map/ppermute | solution.py:56
  210.9 19.4 %copy-start.14 = (bf16[128,2,1024]{2,0,1:T(8,128)(2,1)}, bf16[128,2,1024]{2,0,1:T(8,128)(2,1)S(1)}, u32[]{:S(2)}) copy-start(bf16[128,2,1024]{2,0,1:T(8,128)(2,1)S(1)} %collective-permute-done.6) | copy-start | bytes 1572868
  210.9 14.2 %collective-permute-start.8 = (bf16[128,2,1024]{2,0,1:T(8,128)(2,1)S(1)}, bf16[128,2,1024]{2,0,1:T(8,128)(2,1)}, u32[]{:S(2)}, u32[]{:S(2)}) collective-permute-start(bf16[128,2,1024]{2,0,1:T(8,128)(2,1)S(1)} %collective-permute-done.6), channel_id=1, source_target_pairs={{0,15},{1,0},{2,1},{3,2},{4,3},{5,4},{6,5},{7,6},{8,7},{9,8},{10,9... | collective-permute-start | bytes 1572872 | tf_op jit(solution)/shard_map/ppermute | solution.py:58
  215.7 14.6 %copy-start.7 = (bf16[128,2,1024]{2,0,1:T(8,128)(2,1)}, bf16[128,2,1024]{2,0,1:T(8,128)(2,1)S(1)}, u32[]{:S(2)}) copy-start(bf16[128,2,1024]{2,0,1:T(8,128)(2,1)S(1)} %collective-permute-done.9) | copy-start | bytes 1572868
  215.7 14.6 %collective-permute-start.11 = (bf16[128,2,1024]{2,0,1:T(8,128)(2,1)S(1)}, bf16[128,2,1024]{2,0,1:T(8,128)(2,1)S(1)}, u32[]{:S(2)}, u32[]{:S(2)}) collective-permute-start(bf16[128,2,1024]{2,0,1:T(8,128)(2,1)S(1)} %collective-permute-done.9), channel_id=1, source_target_pairs={{0,1},{1,2},{2,3},{3,4},{4,5},{5,6},{6,7},{7,8},{8,9},{9,10},{10,1... | collective-permute-start | bytes 1572872 | tf_op jit(solution)/shard_map/ppermute | solution.py:56
  225.1 14.3 %collective-permute-start.10 = (bf16[128,2,1024]{2,0,1:T(8,128)(2,1)}, bf16[128,2,1024]{2,0,1:T(8,128)(2,1)}, u32[]{:S(2)}, u32[]{:S(2)}) collective-permute-start(bf16[128,2,1024]{2,0,1:T(8,128)(2,1)} %collective-permute-done.8), channel_id=1, source_target_pairs={{0,15},{1,0},{2,1},{3,2},{4,3},{5,4},{6,5},{7,6},{8,7},{9,8},{10,9... | collective-permute-start | bytes 1572872 | tf_op jit(solution)/shard_map/ppermute | solution.py:58
  230.3 9.2 %copy-start.4 = (bf16[128,2,1024]{2,0,1:T(8,128)(2,1)}, bf16[128,2,1024]{2,0,1:T(8,128)(2,1)S(1)}, u32[]{:S(2)}) copy-start(bf16[128,2,1024]{2,0,1:T(8,128)(2,1)S(1)} %collective-permute-done.11) | copy-start | bytes 1572868
  230.3 14.2 %collective-permute-start.13 = (bf16[128,2,1024]{2,0,1:T(8,128)(2,1)S(1)}, bf16[128,2,1024]{2,0,1:T(8,128)(2,1)S(1)}, u32[]{:S(2)}, u32[]{:S(2)}) collective-permute-start(bf16[128,2,1024]{2,0,1:T(8,128)(2,1)S(1)} %collective-permute-done.11), channel_id=1, source_target_pairs={{0,1},{1,2},{2,3},{3,4},{4,5},{5,6},{6,7},{7,8},{8,9},{9,10},{10,1... | collective-permute-start | bytes 1572872 | tf_op jit(solution)/shard_map/ppermute | solution.py:56
  239.4 20.2 %collective-permute-start.12 = (bf16[128,2,1024]{2,0,1:T(8,128)(2,1)}, bf16[128,2,1024]{2,0,1:T(8,128)(2,1)}, u32[]{:S(2)}, u32[]{:S(2)}) collective-permute-start(bf16[128,2,1024]{2,0,1:T(8,128)(2,1)} %collective-permute-done.10), channel_id=1, source_target_pairs={{0,15},{1,0},{2,1},{3,2},{4,3},{5,4},{6,5},{7,6},{8,7},{9,8},{10,9... | collective-permute-start | bytes 1572872 | tf_op jit(solution)/shard_map/ppermute | solution.py:58
  244.6 16.4 %collective-permute-start.14 = (bf16[128,2,1024]{2,0,1:T(8,128)(2,1)S(1)}, bf16[128,2,1024]{2,0,1:T(8,128)(2,1)S(1)}, u32[]{:S(2)}, u32[]{:S(2)}) collective-permute-start(bf16[128,2,1024]{2,0,1:T(8,128)(2,1)S(1)} %collective-permute-done.13), channel_id=1, source_target_pairs={{0,1},{1,2},{2,3},{3,4},{4,5},{5,6},{6,7},{7,8},{8,9},{9,10},{10,1... | collective-permute-start | bytes 1572872 | tf_op jit(solution)/shard_map/ppermute | solution.py:56
  248.0 3.0 copy-start.2
  251.6 1.0 copy-start.9
  252.7 1.0 copy-start.11
  253.7 1.0 copy-start.13
  254.8 1.0 copy-start.15
  256.1 1.4 copy-start.5
  314.1 1.4 copy-start.1
Sparse Core Ops, SparseCore 0:
  10.1 77.0 all-gather.3
  88.7 31.6 all-gather.5
  122.6 33.0 all-gather.7
  165.6 50.6 reduce-scatter.1
